TPU v7x, 256 devices: a whole 4x4x8 slice. The times are simulated.
256 devices in a mesh: tok: 64 (over z, y, core), unit: 4 (over x).
Axes of the slice: x: 4, y: 4, z: 8, core: 2. Of those that a mesh axis runs over, the one named last changes fastest.
Arguments:
- act_a: bfloat16 [131072, 3072], P('tok', 'unit'), may hold values from -4000 to 4000
- act_b: bfloat16 [131072, 3072], P(('tok', 'unit')), may hold values from -4000 to 4000
Outputs:
- correlation: float32 [3072, 3072], P('tok', 'unit')
All inputs are finite; a program needn't handle non-finite values.
Results may differ from a plain program's by a relative error of at most 0.0003.
Values may be sent and summed in bfloat16 or wider, within the bound.
No kernel may reach another device: no remote copies, remote signals or barrier semaphores. Data moves between devices by JAX's collectives and lax.ppermute only.
A program may use at most 128 MiB of HBM per device.

v0:
```python
import functools
import jax
import jax.numpy as jnp
from jax import lax
from jax.sharding import Mesh
from jax.sharding import PartitionSpec as P

TOK = ("tok_0", "tok_1", "tok_2")
TOK_UNIT = ("tok_0", "tok_1", "tok_2", "unit")


def by_axis(array, axes):
    return functools.reduce(lax.psum, axes, array)


def contract_tokens(left, right):
    return lax.dot_general(
        left, right, (((0,), (0,)), ((), ())), preferred_element_type=jnp.float32
    )


def per_device(act_a, act_b):
    token_rows, own_units = act_a.shape
    units = act_b.shape[1]
    groups = lax.axis_size(TOK)
    band = units // groups
    total_tokens = token_rows * groups
    wide_a = act_a.astype(jnp.float32)
    first_total = jnp.sum(wide_a, axis=0)
    first_square = jnp.sum(wide_a * wide_a, axis=0)
    piece = lax.all_gather(act_b, "unit", axis=0, tiled=True)
    product = contract_tokens(piece, act_a)
    wide_piece = piece.astype(jnp.float32)
    second_total = jnp.sum(wide_piece, axis=0)
    second_square = jnp.sum(wide_piece * wide_piece, axis=0)
    product, second_total, second_square = (product, second_total, second_square)
    shares = lax.psum_scatter(product, TOK, scatter_dimension=0, tiled=True)
    first_all, first_square_all, second_all, second_square_all = (
        by_axis(first_total, TOK),
        by_axis(first_square, TOK),
        by_axis(second_total, TOK),
        by_axis(second_square, TOK),
    )
    offset = lax.axis_index(TOK) * band
    second_own = lax.dynamic_slice_in_dim(second_all, offset, band, 0)
    second_square_own = lax.dynamic_slice_in_dim(second_square_all, offset, band, 0)
    mean_a = first_all / total_tokens
    var_a = first_square_all / total_tokens - mean_a * mean_a
    mean_b = second_own / total_tokens
    var_b = second_square_own / total_tokens - mean_b * mean_b
    centered = shares / total_tokens - mean_b[:, None] * mean_a[None, :]
    return centered / (jnp.sqrt(var_b + 1e-05)[:, None] * jnp.sqrt(var_a + 1e-05)[None, :])


def solution(mesh):
    torus = Mesh(
        mesh.devices.reshape(8, 4, 2, mesh.shape["unit"]), ("tok_0", "tok_1", "tok_2", "unit")
    )
    placed = (P(TOK, "unit"), P(TOK_UNIT, None))
    return jax.shard_map(
        per_device, mesh=torus, in_specs=placed, out_specs=P(TOK, "unit"), check_vma=False
    )
```

profile of v0, /device:TPU:2, one launch (start us, length us, event | category | flops | bytes accessed | tf_op | source)
XLA Modules:
  0.0 314.8 jit_solution(7686966952882575535)
XLA Ops:
  6.5 0.0 all-gather.2.cloned.1.call-start
  6.5 0.7 all-gather.2.cloned.1.call-update
  7.3 0.0 reduce-scatter.2.cloned.1.call-start
  7.3 125.9 %all-gather.2.cloned.1.call-done = bf16[2048,3072]{1,0:T(8,128)(2,1)} async-done(((bf16[512,3072]{1,0:T(8,128)(2,1)}), bf16[2048,3072]{1,0:T(8,128)(2,1)}) %all-gather.2.cloned.1.call-update) | async-done | bytes 12582928 | tf_op jit(solution)/shard_map/all_gather | solution.py:31
  133.2 16.3 %fusion.2 = f32[3072,768]{1,0:T(8,128)} fusion(bf16[2048,3072]{1,0:T(8,128)(2,1)} %all-gather.2.cloned.1.call-done, bf16[2048,768]{1,0:T(8,128)(2,1)} %param.2), kind=kOutput, calls=%fused_computation.11 | convolution fusion | flops 9663676416 | bytes 25165824 | tf_op jit(solution)/shard_map/dot_general | solution.py:17
  149.5 0.0 copy-start
  149.5 0.0 reduce-scatter.2.cloned.1.call-update
  149.5 1.9 copy-done
  151.4 0.9 convert_reduce_fusion.1
  152.2 8.0 %convert_reduce_fusion = (f32[3072]{0:T(1024)S(1)}, f32[3072]{0:T(1024)S(1)}) fusion(bf16[2048,3072]{1,0:T(8,128)(2,1)} %all-gather.2.cloned.1.call-done), kind=kLoop, calls=%fused_computation.1 | loop fusion | flops 25159680 | bytes 12607488 | tf_op jit(solution)/shard_map/reduce_sum | solution.py:34
  160.2 30.2 %all-reduce = (f32[768]{0:T(1024)S(1)}, f32[768]{0:T(1024)S(1)}, f32[3072]{0:T(1024)S(1)}, f32[3072]{0:T(1024)S(1)}) all-reduce(f32[768]{0:T(1024)S(1)} %get-tuple-element.8, f32[768]{0:T(1024)S(1)} %get-tuple-element.7, f32[3072]{0:T(1024)S(1)} %get-tuple-element.6, ...), channel_id=1, replica_groups=mesh['tok_0'=8,'tok_1'=4,'tok_2'=2,'unit'=4] {'tok_0'}, use_global_device_ids=true, to_apply=%region_14.0 | all-reduce | flops 7680 | bytes 61440 | tf_op jit(solution)/shard_map/psum | solution.py:13
  190.4 17.1 %all-reduce.1 = (f32[768]{0:T(1024)S(1)}, f32[768]{0:T(1024)S(1)}, f32[3072]{0:T(1024)S(1)}, f32[3072]{0:T(1024)S(1)}) all-reduce(f32[768]{0:T(1024)S(1)} %get-tuple-element.9, f32[768]{0:T(1024)S(1)} %get-tuple-element.10, f32[3072]{0:T(1024)S(1)} %get-tuple-element.11, ...), channel_id=1, replica_groups=mesh['tok_0'=8,'tok_1'=4,'tok_2'=2,'unit'=4] {'tok_1'}, use_global_device_ids=true, to_apply=%region_15.0 | all-reduce | flops 7680 | bytes 61440 | tf_op jit(solution)/shard_map/psum | solution.py:13
  207.5 3.4 %all-reduce.2 = (f32[768]{0:T(1024)S(1)}, f32[768]{0:T(1024)S(1)}, f32[3072]{0:T(1024)S(1)}, f32[3072]{0:T(1024)S(1)}) all-reduce(f32[768]{0:T(1024)S(1)} %get-tuple-element.13, f32[768]{0:T(1024)S(1)} %get-tuple-element.14, f32[3072]{0:T(1024)S(1)} %get-tuple-element.15, ...), channel_id=1, replica_groups=mesh['tok_0'=8,'tok_1'=4,'tok_2'=2,'unit'=4] {'tok_2'}, use_global_device_ids=true, to_apply=%region_16.0 | all-reduce | flops 7680 | bytes 61440 | tf_op jit(solution)/shard_map/psum | solution.py:13
  210.9 0.1 dynamic-slice_multiply_fusion
  211.0 95.2 %reduce-scatter.2.cloned.1.call-done = f32[48,768]{1,0:T(8,128)} async-done(((f32[3072,768]{1,0:T(8,128)}), f32[48,768]{1,0:T(8,128)}) %reduce-scatter.2.cloned.1.call-update) | async-done | bytes 147472 | tf_op jit(solution)/shard_map/reduce_scatter | solution.py:37
  306.3 1.7 multiply_divide_fusion
  (1 shorter events, 0.0 us)
Async XLA Ops:
  6.5 126.7 %all-gather.2.cloned.1.call-start = ((), (), s32[]{:S(2)}) async-start(), calls=%async_computation.1 | async-start | bytes 15728640 | tf_op jit(solution)/shard_map/all_gather | solution.py:31
  7.3 299.0 %reduce-scatter.2.cloned.1.call-start = ((), (), s32[]{:S(2)}) async-start(), calls=%async_computation.2 | async-start | bytes 9584640 | tf_op jit(solution)/shard_map/reduce_scatter | solution.py:37
  149.5 1.9 copy-start
Sparse Core Ops, SparseCore 0:
  9.1 124.0 all-gather.1
  149.6 156.6 reduce-scatter.1
where the time goes:
time: 315 us
  waiting for transfers between devices  222 us (70%)
  blocking collectives  50.7 us (16%)
  matrix products  16.3 us (5%)
  between operations  13.4 us (4%)
  other arithmetic  10.6 us (3%)
    all_gather x1, waiting for transfers between devices, per_device(): piece = lax.all_gather(act_b, 'unit', axis=0, tiled=True)  126 us
    reduce_scatter x1, waiting for transfers between devices, per_device(): shares = lax.psum_scatter(product, TOK, scatter_dimension=0, tiled=True)  95.2 us
    psum x3, blocking collectives, by_axis(): return functools.reduce(lax.psum, axes, array)  50.7 us
    dot_general x1, matrix products, contract_tokens(): lax.dot_general(left, right, (((0,), (0,)), ((), ())), preferred_element_...  16.3 us
    reduce_sum x1, other arithmetic, per_device(): second_total = jnp.sum(wide_piece, axis=0)  7.99 us
  transfers between devices with their start and end apart: 2, of which 2 were waited for; matrix products, arithmetic and copies ran while one was open for 3% of the time, Pallas kernels for 0%

commit v1 on v0

--- a/solution.py
+++ b/solution.py
@@ -7,6 +7,27 @@
 
 TOK = ("tok_0", "tok_1", "tok_2")
 TOK_UNIT = ("tok_0", "tok_1", "tok_2", "unit")
+
+
+def gather_around(value, axis, dim):
+    size, index, extent = (lax.axis_size(axis), lax.axis_index(axis), value.shape[dim])
+    right = [(i, (i + 1) % size) for i in range(size)]
+    left = [(i, (i - 1) % size) for i in range(size)]
+    out = jnp.zeros((*value.shape[:dim], size * extent, *value.shape[dim + 1 :]), value.dtype)
+    out = lax.dynamic_update_slice_in_dim(out, value, index * extent, axis=dim)
+    from_left = from_right = value
+    half = size // 2
+    for lap in range(1, half + 1):
+        from_left = lax.ppermute(from_left, axis, right)
+        out = lax.dynamic_update_slice_in_dim(
+            out, from_left, (index - lap) % size * extent, axis=dim
+        )
+        if lap < size - half:
+            from_right = lax.ppermute(from_right, axis, left)
+            out = lax.dynamic_update_slice_in_dim(
+                out, from_right, (index + lap) % size * extent, axis=dim
+            )
+    return out
 
 
 def by_axis(array, axes):
@@ -28,7 +49,7 @@
     wide_a = act_a.astype(jnp.float32)
     first_total = jnp.sum(wide_a, axis=0)
     first_square = jnp.sum(wide_a * wide_a, axis=0)
-    piece = lax.all_gather(act_b, "unit", axis=0, tiled=True)
+    piece = gather_around(act_b, "unit", 0)
     product = contract_tokens(piece, act_a)
     wide_piece = piece.astype(jnp.float32)
     second_total = jnp.sum(wide_piece, axis=0)

time: 315 us -> 333 us (1.057)
  local copies, waits for them, and re-layouts: 1.85 us -> 19.5 us
  waiting for transfers between devices: 222 us -> 216 us
  starting transfers between devices: 0.04 us -> 3.74 us
    all_gather x1 -> x0, waiting for transfers between devices: 126 us -> none  [per_device(): piece = lax.all_gather(act_b, 'unit', axis=0, tiled=True)]
    ppermute x0 -> x3, waiting for transfers between devices: none -> 120 us  [the longest x2 120 us: gather_around(): from_left = lax.ppermute(from_left, axis, right)]
    dynamic_update_slice x0 -> x4, local copies, waits for them, and re-layouts: none -> 13.3 us  [the longest x2 7.65 us: gather_around(): lax.dynamic_update_slice_in_dim(out, from_left, (index - lap) % size * ex...]
    broadcast_in_dim x0 -> x1, local copies, waits for them, and re-layouts: none -> 6.16 us  [gather_around(): jnp.zeros((*value.shape[:dim], size * extent, *value.shape[dim + 1:]), va...]
    ppermute x0 -> x3, starting transfers between devices: none -> 3.74 us  [the longest x2 2.98 us: gather_around(): from_left = lax.ppermute(from_left, axis, right)]
  transfers between devices with their start and end apart: 2 -> 4, of which waited for: 2 -> 3; matrix products, arithmetic and copies ran while one was open for 3% -> 7% of each run, Pallas kernels for 0% -> 0%
where the time goes in v1:
time: 333 us; the launch traced here: 332 us
  waiting for transfers between devices  216 us (65%)
  blocking collectives  53.8 us (16%)
  local copies, waits for them, and re-layouts  19.5 us (6%)
  matrix products  15.4 us (5%)
  between operations  13.4 us (4%)
  other arithmetic  10.6 us (3%)
  starting transfers between devices  3.74 us (1%)
    ppermute x2, waiting for transfers between devices, gather_around(): from_left = lax.ppermute(from_left, axis, right)  120 us
    reduce_scatter x1, waiting for transfers between devices, per_device(): shares = lax.psum_scatter(product, TOK, scatter_dimension=0, tiled=True)  96.2 us
    psum x3, blocking collectives, by_axis(): return functools.reduce(lax.psum, axes, array)  53.8 us
    dot_general x1, matrix products, contract_tokens(): lax.dot_general(left, right, (((0,), (0,)), ((), ())), preferred_element_...  15.4 us
    reduce_sum x1, other arithmetic, per_device(): second_total = jnp.sum(wide_piece, axis=0)  8 us
    dynamic_update_slice x2, local copies, waits for them, and re-layouts, gather_around(): lax.dynamic_update_slice_in_dim(out, from_left, (index - lap) % size * ex...  7.65 us
  transfers between devices with their start and end apart: 4, of which 3 were waited for; matrix products, arithmetic and copies ran while one was open for 7% of the time, Pallas kernels for 0%

profile of v1, /device:TPU:2, one launch (start us, length us, event | category | flops | bytes accessed | tf_op | source)
XLA Modules:
  0.0 332.4 jit_solution(5492814164894126894)
XLA Ops:
  6.5 0.0 copy-start
  6.5 0.0 reduce-scatter.2.cloned.1.call-start
  6.5 1.5 collective-permute-start
  8.0 0.8 collective-permute-start.1
  8.8 67.9 %collective-permute-done = bf16[512,3072]{1,0:T(8,128)(2,1)} collective-permute-done((bf16[512,3072]{1,0:T(8,128)(2,1)}, bf16[512,3072]{1,0:T(8,128)(2,1)}, u32[]{:S(2)}, u32[]{:S(2)}) %collective-permute-start) | collective-permute-done | bytes 3145760 | tf_op jit(solution)/shard_map/ppermute | solution.py:21
  76.7 1.5 collective-permute-start.2
  78.2 6.2 %broadcast_in_dim.2 = bf16[2048,3072]{1,0:T(8,128)(2,1)} broadcast(bf16[]{:T(256)} %constant.52.clone.1), dimensions={} | broadcast | bytes 12582914 | tf_op jit(solution)/shard_map/broadcast_in_dim | solution.py:16
  84.4 0.0 copy-done
  84.4 0.0 copy-start.1
  84.4 1.9 constant_dynamic-update-slice_fusion.3
  86.3 3.9 %constant_dynamic-update-slice_fusion.2 = bf16[2048,3072]{1,0:T(8,128)(2,1)} fusion(bf16[2048,3072]{1,0:T(8,128)(2,1)} %constant_dynamic-update-slice_fusion.3, bf16[512,3072]{1,0:T(8,128)(2,1)} %collective-permute-done, s32[]{:T(128)S(6)} %select_n.33), kind=kLoop, calls=%fused_computation.11 | loop fusion | bytes 6291460 | tf_op jit(solution)/shard_map/dynamic_update_slice | solution.py:22
  90.2 0.0 collective-permute-done.1
  90.2 3.8 %constant_dynamic-update-slice_fusion.1 = bf16[2048,3072]{1,0:T(8,128)(2,1)} fusion(bf16[2048,3072]{1,0:T(8,128)(2,1)} %constant_dynamic-update-slice_fusion.2, bf16[512,3072]{1,0:T(8,128)(2,1)} %collective-permute-done.1, s32[]{:T(128)S(6)} %select_n.35), kind=kLoop, calls=%fused_computation.10 | loop fusion | bytes 6291460 | tf_op jit(solution)/shard_map/dynamic_update_slice | solution.py:27
  94.0 51.7 %collective-permute-done.2 = bf16[512,3072]{1,0:T(8,128)(2,1)} collective-permute-done((bf16[512,3072]{1,0:T(8,128)(2,1)}, bf16[512,3072]{1,0:T(8,128)(2,1)}, u32[]{:S(2)}, u32[]{:S(2)}) %collective-permute-start.2) | collective-permute-done | bytes 3145760 | tf_op jit(solution)/shard_map/ppermute | solution.py:21
  145.7 3.7 %constant_dynamic-update-slice_fusion = bf16[2048,3072]{1,0:T(8,128)(2,1)} fusion(bf16[2048,3072]{1,0:T(8,128)(2,1)} %constant_dynamic-update-slice_fusion.1, bf16[512,3072]{1,0:T(8,128)(2,1)} %collective-permute-done.2, s32[]{:T(128)S(6)} %select_n.37), kind=kLoop, calls=%fused_computation.9 | loop fusion | bytes 6291460 | tf_op jit(solution)/shard_map/dynamic_update_slice | solution.py:22
  149.4 0.0 copy-done.1
  149.4 0.0 copy-start.2
  149.4 15.4 %fusion.2 = f32[3072,768]{1,0:T(8,128)} fusion(bf16[2048,3072]{1,0:T(8,128)(2,1)} %constant_dynamic-update-slice_fusion, bf16[2048,768]{1,0:T(8,128)(2,1)S(1)} %copy-done.1), kind=kOutput, calls=%fused_computation.15 | convolution fusion | flops 9663676416 | bytes 25165824 | tf_op jit(solution)/shard_map/dot_general | solution.py:38
  164.9 0.0 reduce-scatter.2.cloned.1.call-update
  164.9 0.0 copy-done.2
  164.9 0.9 convert_reduce_fusion.1
  165.8 8.0 %convert_reduce_fusion = (f32[3072]{0:T(1024)S(1)}, f32[3072]{0:T(1024)S(1)}) fusion(bf16[2048,3072]{1,0:T(8,128)(2,1)} %constant_dynamic-update-slice_fusion), kind=kLoop, calls=%fused_computation.1 | loop fusion | flops 25159680 | bytes 12607488 | tf_op jit(solution)/shard_map/reduce_sum | solution.py:55
  173.8 33.1 %all-reduce = (f32[768]{0:T(1024)S(1)}, f32[768]{0:T(1024)S(1)}, f32[3072]{0:T(1024)S(1)}, f32[3072]{0:T(1024)S(1)}) all-reduce(f32[768]{0:T(1024)S(1)} %get-tuple-element.8, f32[768]{0:T(1024)S(1)} %get-tuple-element.7, f32[3072]{0:T(1024)S(1)} %get-tuple-element.6, ...), channel_id=1, replica_groups=mesh['tok_0'=8,'tok_1'=4,'tok_2'=2,'unit'=4] {'tok_0'}, use_global_device_ids=true, to_apply=%region_14.15 | all-reduce | flops 7680 | bytes 61440 | tf_op jit(solution)/shard_map/psum | solution.py:34
  206.8 17.3 %all-reduce.1 = (f32[768]{0:T(1024)S(1)}, f32[768]{0:T(1024)S(1)}, f32[3072]{0:T(1024)S(1)}, f32[3072]{0:T(1024)S(1)}) all-reduce(f32[768]{0:T(1024)S(1)} %get-tuple-element.9, f32[768]{0:T(1024)S(1)} %get-tuple-element.10, f32[3072]{0:T(1024)S(1)} %get-tuple-element.11, ...), channel_id=1, replica_groups=mesh['tok_0'=8,'tok_1'=4,'tok_2'=2,'unit'=4] {'tok_1'}, use_global_device_ids=true, to_apply=%region_15.16 | all-reduce | flops 7680 | bytes 61440 | tf_op jit(solution)/shard_map/psum | solution.py:34
  224.1 3.4 %all-reduce.2 = (f32[768]{0:T(1024)S(1)}, f32[768]{0:T(1024)S(1)}, f32[3072]{0:T(1024)S(1)}, f32[3072]{0:T(1024)S(1)}) all-reduce(f32[768]{0:T(1024)S(1)} %get-tuple-element.13, f32[768]{0:T(1024)S(1)} %get-tuple-element.14, f32[3072]{0:T(1024)S(1)} %get-tuple-element.15, ...), channel_id=1, replica_groups=mesh['tok_0'=8,'tok_1'=4,'tok_2'=2,'unit'=4] {'tok_2'}, use_global_device_ids=true, to_apply=%region_16.17 | all-reduce | flops 7680 | bytes 61440 | tf_op jit(solution)/shard_map/psum | solution.py:34
  227.6 0.1 dynamic-slice_multiply_fusion
  227.7 96.2 %reduce-scatter.2.cloned.1.call-done = f32[48,768]{1,0:T(8,128)} async-done(((f32[3072,768]{1,0:T(8,128)}), f32[48,768]{1,0:T(8,128)}) %reduce-scatter.2.cloned.1.call-update) | async-done | bytes 147472 | tf_op jit(solution)/shard_map/reduce_scatter | solution.py:58
  323.9 1.7 multiply_divide_fusion
  (1 shorter events, 0.0 us)
Async XLA Ops:
  6.5 77.8 %copy-start = (bf16[512,3072]{1,0:T(8,128)(2,1)S(1)}, bf16[512,3072]{1,0:T(8,128)(2,1)}, u32[]{:S(2)}) copy-start(bf16[512,3072]{1,0:T(8,128)(2,1)} %param.3) | copy-start | bytes 9437188
  6.5 317.4 %reduce-scatter.2.cloned.1.call-start = ((), (), s32[]{:S(2)}) async-start(), calls=%async_computation.1 | async-start | bytes 9584640 | tf_op jit(solution)/shard_map/reduce_scatter | solution.py:58
  6.5 70.2 %collective-permute-start = (bf16[512,3072]{1,0:T(8,128)(2,1)}, bf16[512,3072]{1,0:T(8,128)(2,1)}, u32[]{:S(2)}, u32[]{:S(2)}) collective-permute-start(bf16[512,3072]{1,0:T(8,128)(2,1)} %param.3), channel_id=1, source_target_pairs={{0,1},{1,2},{2,3},{3,0},{4,5},{5,6},{6,7},{7,4},{8,9},{9,10},{10,1... | collective-permute-start | bytes 9437192 | tf_op jit(solution)/shard_map/ppermute | solution.py:21
  8.0 82.2 %collective-permute-start.1 = (bf16[512,3072]{1,0:T(8,128)(2,1)}, bf16[512,3072]{1,0:T(8,128)(2,1)}, u32[]{:S(2)}, u32[]{:S(2)}) collective-permute-start(bf16[512,3072]{1,0:T(8,128)(2,1)} %param.3), channel_id=1, source_target_pairs={{0,3},{1,0},{2,1},{3,2},{4,7},{5,4},{6,5},{7,6},{8,11},{9,8},{10,9... | collective-permute-start | bytes 9437192 | tf_op jit(solution)/shard_map/ppermute | solution.py:26
  76.7 69.0 %collective-permute-start.2 = (bf16[512,3072]{1,0:T(8,128)(2,1)}, bf16[512,3072]{1,0:T(8,128)(2,1)}, u32[]{:S(2)}, u32[]{:S(2)}) collective-permute-start(bf16[512,3072]{1,0:T(8,128)(2,1)} %collective-permute-done), channel_id=1, source_target_pairs={{0,1},{1,2},{2,3},{3,0},{4,5},{5,6},{6,7},{7,4},{8,9},{9,10},{10,1... | collective-permute-start | bytes 9437192 | tf_op jit(solution)/shard_map/ppermute | solution.py:21
  84.4 65.1 %copy-start.1 = (bf16[2048,768]{1,0:T(8,128)(2,1)S(1)}, bf16[2048,768]{1,0:T(8,128)(2,1)}, u32[]{:S(2)}) copy-start(bf16[2048,768]{1,0:T(8,128)(2,1)} %param.2) | copy-start | bytes 9437188
  149.4 15.5 %copy-start.2 = (bf16[2048,768]{1,0:T(8,128)(2,1)S(1)}, bf16[2048,768]{1,0:T(8,128)(2,1)}, u32[]{:S(2)}) copy-start(bf16[2048,768]{1,0:T(8,128)(2,1)} %param.2) | copy-start | bytes 9437188
Sparse Core Ops, SparseCore 0:
  165.0 158.8 reduce-scatter.1
